TPU v7x, 32 devices: a whole 2x2x4 slice. The times are simulated.
32 devices in a mesh: tm: 4 (over y, x), lat: 4 (over z), ens: 2 (over core).
Axes of the slice: x: 2, y: 2, z: 4, core: 2. Of those that a mesh axis runs over, the one named last changes fastest.
Arguments:
- increment: float32 [4, 4, 64, 1440], P('tm', None, 'lat'), may hold values from -6 to 6
- wind_lon: float32 [4, 4, 64, 1440], P('tm', None, 'lat'), may hold values from -0.45 to 0.45
- wind_lat: float32 [4, 4, 64, 1440], P('tm', None, 'lat'), may hold values from -0.45 to 0.45
- model_precision: float32 [4], replicated, may hold values from 0.5 to 4
- perturbations: float32 [32, 4, 64, 1440], P('ens', 'tm', 'lat'), may hold values from -0.24350093 to 0.24350093
- obs_rows: int32 [4, 128], P('tm', 'lat'), may hold values from 0 to 63
- obs_jacobian: float32 [4, 128, 16, 1440], P('tm', 'lat'), may hold values from -0.15625 to 0.15625
- obs_values: float32 [4, 128, 16], P('tm', 'lat'), may hold values from -6 to 6
- obs_precision: float32 [4, 128, 16], P('tm', 'lat'), may hold values from 0.5 to 2
- obs_counts: int32 [4, 128], P('tm', 'lat'), may hold values from 1 to 16
Outputs:
- grad_state: float32 [4, 4, 64, 1440], P('tm', None, 'lat')
- forcing_step: float32 [4, 64, 1440], P('tm', 'lat')
Inputs may be any that keep to these rules, and one draw needn't show every extreme that they name: `obs_rows`: block j of band b reads level r // 16 and latitude b * 16 + r % 16, where r is its entry; several blocks may read the same row. `obs_counts`: only the first count slots of a block hold observations.
All inputs are finite; a program needn't handle non-finite values.
Results may differ from a plain program's by a relative error of at most 0.0003.
Values sent between devices are 32-bit elements; how exact they have to be, the bound alone decides.
A program may use at most 64 MiB of HBM per device.

v0:
```python
import jax
import jax.numpy as jnp
from jax import lax
from jax.sharding import PartitionSpec as P

MEM = 32
STEPS = 4


def padded(value, sides, width):
    for axis, dim in sides:
        peers, length = (lax.axis_size(axis), value.shape[dim])
        up = [(i, (i + 1) % peers) for i in range(peers - 1)]
        down = [(j, i) for i, j in up]
        last = lax.slice_in_dim(value, length - width, length, axis=dim)
        leading = lax.slice_in_dim(value, 0, width, axis=dim)
        before = lax.ppermute(last, axis, up)
        after = lax.ppermute(leading, axis, down)
        value = jnp.concatenate([before, value, after], axis=dim)
    return value


def shifted(value, axis, steps):
    count = lax.axis_size(axis)
    leading, last = (max(0, -steps), min(count, count - steps))
    return lax.ppermute(value, axis, [(source, source + steps) for source in range(leading, last)])


def coefficients(wind_lon, wind_lat):
    center = 1.0 - wind_lon * wind_lon - wind_lat * wind_lat
    plus_lon = 0.5 * (wind_lon * wind_lon - wind_lon)
    minus_lon = 0.5 * (wind_lon * wind_lon + wind_lon)
    plus_lat = 0.5 * (wind_lat * wind_lat - wind_lat)
    minus_lat = 0.5 * (wind_lat * wind_lat + wind_lat)
    return (center, plus_lon, minus_lon, plus_lat, minus_lat)


def trim_coefs(coefs, first, last):
    return tuple((item[:, first:last] for item in coefs))


def advect_inner(field, coefs):
    center, plus_lon, minus_lon, plus_lat, minus_lat = trim_coefs(coefs, 1, coefs[0].shape[1] - 1)
    middle = field[:, 1:-1]
    return (
        center * middle
        + plus_lon * jnp.roll(middle, -1, 2)
        + minus_lon * jnp.roll(middle, 1, 2)
        + plus_lat * field[:, 2:]
        + minus_lat * field[:, :-2]
    )


def adjoint_inner(field, coefs):
    center, plus_lon, minus_lon, plus_lat, minus_lat = coefs
    middle = field[:, 1:-1]
    inner_plus = plus_lon[:, 1:-1]
    inner_minus = minus_lon[:, 1:-1]
    from_south = (plus_lat * field)[:, :-2]
    from_north = (minus_lat * field)[:, 2:]
    return (
        center[:, 1:-1] * middle
        + jnp.roll(inner_plus * middle, 1, 2)
        + jnp.roll(inner_minus * middle, -1, 2)
        + from_south
        + from_north
    )


def on_device(
    increment,
    wind_lon,
    wind_lat,
    model_precision,
    perturbations,
    obs_rows,
    obs_jacobian,
    obs_values,
    obs_precision,
    obs_counts,
):
    highest = lax.Precision.HIGHEST
    level_prec = model_precision[:, None, None]
    band_rows = increment.shape[2]
    stacked = jnp.stack([increment[0], wind_lon[0], wind_lat[0]])
    widened = padded(stacked, (("lat", 2),), STEPS)
    wide_coefs = coefficients(widened[1], widened[2])
    width = widened.shape[2]
    field = widened[0]
    for repeat in range(STEPS):
        field = advect_inner(field, trim_coefs(wide_coefs, repeat, width - repeat))
    prior = shifted(field, "tm", 1)
    mismatch = level_prec * (increment[0] - prior)
    later = shifted(mismatch, "tm", -1)
    levels, lat_rows, lon_cells = field.shape
    flat = field.reshape(levels * lat_rows, lon_cells)
    row_ids = jnp.arange(levels * lat_rows, dtype=jnp.int32)
    onehot = (obs_rows[0][:, None] == row_ids[None, :]).astype(jnp.float32)
    picked = jnp.dot(onehot, flat, precision=highest)
    jacobian = obs_jacobian[0]
    evolved = jnp.einsum("jon,jn->jo", jacobian, picked, precision=highest)
    slots = jnp.arange(jacobian.shape[1], dtype=jnp.int32)
    used = (slots[None, :] < obs_counts[0][:, None]).astype(jnp.float32)
    weighted = obs_precision[0] * (evolved - obs_values[0]) * used
    force = jnp.einsum("jon,jo->jn", jacobian, weighted, precision=highest)
    placed = jnp.dot(onehot.T, force, precision=highest).reshape(levels, lat_rows, lon_cells)
    adjoint = placed - later
    forcing = adjoint
    spread = padded(adjoint[None], (("lat", 2),), STEPS)[0]
    for repeat in range(STEPS):
        spread = adjoint_inner(spread, trim_coefs(wide_coefs, repeat, width - repeat))
        if repeat + 1 < STEPS:
            offset = STEPS - repeat - 1
            forcing = forcing + spread[:, offset : offset + band_rows]
    adjoint = spread
    grad_state = (adjoint + mismatch)[None]
    reduced = lax.psum_scatter(forcing, "tm", scatter_dimension=0, tiled=True)
    local_coef = jnp.einsum("mlan,lan->m", perturbations, reduced, precision=highest)
    member_coef = lax.psum(local_coef, ("tm", "lat"))
    every_member, every_coef = (
        lax.all_gather(perturbations, "ens", axis=0, tiled=True),
        lax.all_gather(member_coef, "ens", axis=0, tiled=True),
    )
    combined = jnp.einsum("m,mlan->lan", every_coef, every_member, precision=highest)
    forcing_step = -combined / (MEM - 1.0)
    return (grad_state, forcing_step)


def solution(mesh):
    placed = (
        P("tm", None, "lat", None),
        P("tm", None, "lat", None),
        P("tm", None, "lat", None),
        P(),
        P("ens", "tm", "lat", None),
        P("tm", "lat"),
        P("tm", "lat", None, None),
        P("tm", "lat", None),
        P("tm", "lat", None),
        P("tm", "lat"),
    )
    return jax.shard_map(
        on_device,
        mesh=mesh,
        in_specs=placed,
        out_specs=(P("tm", None, "lat", None), P("tm", "lat", None)),
        check_vma=False,
    )
```

profile of v0, /device:TPU:0, one launch (start us, length us, event | category | flops | bytes accessed | tf_op | source)
XLA Modules:
  0.0 158.9 jit_solution(5019964495041430061)
XLA Ops:
  10.5 5.0 %collective-permute-start = (f32[3,4,4,1440]{3,2,1,0:T(4,128)S(1)}, f32[3,4,4,1440]{3,2,1,0:T(4,128)S(1)}, u32[]{:S(2)}, u32[]{:S(2)}) collective-permute-start(f32[3,4,4,1440]{3,2,1,0:T(4,128)S(1)} %get-tuple-element.7), channel_id=1, source_target_pairs={{0,2},{2,4},{4,6},{1,3},{3,5},{5,7},{8,10},{10,12},{12,14},{9,11},... | collective-permute-start | bytes 829448 | tf_op jit(solution)/shard_map/ppermute | solution.py:17
  15.4 1.3 collective-permute-start.1
  16.7 4.9 %collective-permute-done = f32[3,4,4,1440]{3,2,1,0:T(4,128)S(1)} collective-permute-done((f32[3,4,4,1440]{3,2,1,0:T(4,128)S(1)}, f32[3,4,4,1440]{3,2,1,0:T(4,128)S(1)}, u32[]{:S(2)}, u32[]{:S(2)}) %collective-permute-start) | collective-permute-done | bytes 276512 | tf_op jit(solution)/shard_map/ppermute | solution.py:17
  21.7 4.1 %collective-permute-done.1 = f32[3,4,4,1440]{3,2,1,0:T(4,128)S(1)} collective-permute-done((f32[3,4,4,1440]{3,2,1,0:T(4,128)S(1)}, f32[3,4,4,1440]{3,2,1,0:T(4,128)S(1)}, u32[]{:S(2)}, u32[]{:S(2)}) %collective-permute-start.1) | collective-permute-done | bytes 276512 | tf_op jit(solution)/shard_map/ppermute | solution.py:18
  26.9 1.7 %fusion.63 = (f32[4,22,1440]{2,1,0:T(8,128)}, f32[4,22,1440]{2,1,0:T(8,128)S(1)}, f32[4,22,1440]{2,1,0:T(8,128)}) fusion(f32[4,24,1440]{2,1,0:T(8,128)S(1)} %get-tuple-element.2, f32[4,24,1440]{2,1,0:T(8,128)S(1)} %slice_bitcast_fusion, f32[4,24,1440]{2,1,0:T(8,128)S(1)} %get-tuple-element.3, f32[4,22,1439]{2,1,0:T(8,128)S(1)} %get-tuple-element.41, ...), kind=kLoop, calls=%fused_computation.123 | loop fusion | flops 1393920 | bytes 6589440 | tf_op jit(solution)/shard_map/slice | solution.py:39
  28.9 1.7 %fusion.62 = (f32[4,20,1440]{2,1,0:T(8,128)}, f32[4,20,1440]{2,1,0:T(8,128)S(1)}, f32[4,20,1440]{2,1,0:T(8,128)}) fusion(f32[4,24,1440]{2,1,0:T(8,128)S(1)} %get-tuple-element.2, f32[4,22,1440]{2,1,0:T(8,128)S(1)} %get-tuple-element.23, f32[4,24,1440]{2,1,0:T(8,128)S(1)} %get-tuple-element.3, f32[4,20,1439]{2,1,0:T(8,128)S(1)} %get-tuple-element.37, ...), kind=kLoop, calls=%fused_computation.122 | loop fusion | flops 1267200 | bytes 5990400 | tf_op jit(solution)/shard_map/slice | solution.py:39
  31.0 1.7 %fusion.61 = (f32[4,18,1440]{2,1,0:T(8,128)}, f32[4,18,1440]{2,1,0:T(8,128)S(1)}, f32[4,18,1440]{2,1,0:T(8,128)}) fusion(f32[4,24,1440]{2,1,0:T(8,128)S(1)} %get-tuple-element.2, f32[4,20,1440]{2,1,0:T(8,128)S(1)} %get-tuple-element.18, f32[4,24,1440]{2,1,0:T(8,128)S(1)} %get-tuple-element.3, f32[4,18,1439]{2,1,0:T(8,128)S(1)} %get-tuple-element.33, ...), kind=kLoop, calls=%fused_computation.121 | loop fusion | flops 1140480 | bytes 5391360 | tf_op jit(solution)/shard_map/slice | solution.py:39
  33.5 4.2 %collective-permute-start.2 = (f32[4,16,1440]{2,1,0:T(8,128)S(1)}, f32[4,16,1440]{2,1,0:T(8,128)}, u32[]{:S(2)}, u32[]{:S(2)}) collective-permute-start(f32[4,16,1440]{2,1,0:T(8,128)S(1)} %fusion.41), channel_id=1, source_target_pairs={{0,8},{8,16},{16,24},{1,9},{9,17},{17,25},{2,10},{10,18},{18,26},{... | collective-permute-start | bytes 1105928 | tf_op jit(solution)/shard_map/ppermute | solution.py:26
  38.0 3.6 %fusion.2 = f32[32,1,16]{2,1,0:T(1,128)S(1)} fusion(f32[1,32,16,1440]{3,2,1,0:T(8,128)S(1)} %copy-done, f32[32,1440,1]{1,0,2:T(8,128)S(1)} %convolution_bitcast_fusion), kind=kOutput, calls=%fused_computation.2 | convolution fusion | flops 8847360 | bytes 3135488 | tf_op jit(solution)/shard_map/jon,jn->jo/dot_general | solution.py:101
  42.3 1.3 fusion.56
  44.4 1.2 fusion.46
  45.6 1.4 collective-permute-start.3
  47.1 1.6 %fusion = f32[32,1,1440]{2,1,0:T(1,128)S(1)} fusion(f32[32,16,1]{1,2,0:T(1,128)S(1)} %copy.14, f32[1,32,16,1440]{3,2,1,0:T(8,128)S(1)} %copy-done), kind=kOutput, calls=%fused_computation | convolution fusion | flops 8847360 | bytes 3135488 | tf_op jit(solution)/shard_map/jon,jo->jn/dot_general | solution.py:105
  49.2 8.0 %collective-permute-done.3 = f32[4,16,1440]{2,1,0:T(8,128)S(1)} collective-permute-done((f32[4,16,1440]{2,1,0:T(8,128)S(1)}, f32[4,16,1440]{2,1,0:T(8,128)S(1)}, u32[]{:S(2)}, u32[]{:S(2)}) %collective-permute-start.3) | collective-permute-done | bytes 368672 | tf_op jit(solution)/shard_map/ppermute | solution.py:26
  57.2 3.5 %collective-permute-start.4 = (f32[1,4,4,1440]{3,2,1,0:T(4,128)S(1)}, f32[1,4,4,1440]{3,2,1,0:T(4,128)S(1)}, u32[]{:S(2)}, u32[]{:S(2)}) collective-permute-start(f32[1,4,4,1440]{3,2,1,0:T(4,128)S(1)} %get-tuple-element.43), channel_id=1, source_target_pairs={{0,2},{2,4},{4,6},{1,3},{3,5},{5,7},{8,10},{10,12},{12,14},{9,11},... | collective-permute-start | bytes 276488 | tf_op jit(solution)/shard_map/ppermute | solution.py:17
  60.7 1.5 collective-permute-start.5
  62.9 4.3 %collective-permute-done.5 = f32[1,4,4,1440]{3,2,1,0:T(4,128)S(1)} collective-permute-done((f32[1,4,4,1440]{3,2,1,0:T(4,128)S(1)}, f32[1,4,4,1440]{3,2,1,0:T(4,128)S(1)}, u32[]{:S(2)}, u32[]{:S(2)}) %collective-permute-start.5) | collective-permute-done | bytes 92192 | tf_op jit(solution)/shard_map/ppermute | solution.py:18
  72.6 1.2 fusion.36
  76.7 3.2 %fusion.39 = f32[1,4,16,1440]{3,2,1,0:T(8,128)} fusion(f32[4,16,1440]{2,1,0:T(8,128)} %copy-done.16, f32[4,18,1440]{2,1,0:T(8,128)} %copy-done.11, f32[4,18,1440]{2,1,0:T(8,128)} %get-tuple-element.14, f32[4,18,1440]{2,1,0:T(8,128)} %get-tuple-element.12, f32[4,16,1439]{2,1,0:T(8,128)} %bitcast.87, f32[4,16,1]{2,1,0:T(8,128)S(1)} %slice.513, ...), kind=kLoop, calls=%fused_computation.82 | loop fusion | flops 921600 | bytes 3686400 | tf_op jit(solution)/shard_map/broadcast_in_dim | solution.py:116
  79.9 18.2 %reduce-scatter.4.cloned.1.call-done = f32[1,16,1440]{2,1,0:T(8,128)} async-done(((f32[4,16,1440]{2,1,0:T(8,128)}), f32[1,16,1440]{2,1,0:T(8,128)}) %reduce-scatter.4.cloned.1.call-update) | async-done | bytes 92176
  98.1 4.0 %fusion.8 = f32[16]{0:T(128)S(1)} fusion(f32[16,16,1440]{2,1,0:T(8,128)} %bitcast.80, f32[16,1440,1]{1,0,2:T(8,128)} %bitcast.90), kind=kOutput, calls=%fused_computation.16 | convolution fusion | flops 4423680 | bytes 1566784 | tf_op jit(solution)/shard_map/mlan,lan->m/dot_general | solution.py:118
  102.0 41.0 %psum.7 = f32[16]{0:T(128)S(1)} all-reduce(f32[16]{0:T(128)S(1)} %fusion.8), channel_id=1, replica_groups=mesh['tm'=4,'lat'=4,'ens'=2] {'tm','lat'}, use_global_device_ids=true, to_apply=%region_1.2 | all-reduce | flops 16 | bytes 128 | tf_op jit(solution)/shard_map/psum | solution.py:119
  143.3 2.4 %all-reduce = f32[32]{0:T(128)S(1)} all-reduce(f32[32]{0:T(128)S(1)} %dynamic-update-slice), channel_id=1, replica_groups=mesh['tm'=4,'lat'=4,'ens'=2] {'ens'}, use_global_device_ids=true, to_apply=%add | all-reduce | flops 32 | bytes 256
  145.7 5.1 %fusion.4 = f32[1,16,1440]{2,0,1:T(1,128)S(1)} fusion(f32[32,16,1440]{2,1,0:T(8,128)} %bitcast.83, f32[32]{0:T(128)S(1)} %all-reduce), kind=kOutput, calls=%fused_computation.4 | convolution fusion | flops 8847360 | bytes 3041408 | tf_op jit(solution)/shard_map/m,mlan->lan/dot_general | solution.py:124
  (94 shorter events, 16.2 us)
Async XLA Ops:
  8.0 30.0 %copy-start = (f32[1,32,16,1440]{3,2,1,0:T(8,128)S(1)}, f32[1,32,16,1440]{3,2,1,0:T(8,128)}, u32[]{:S(2)}) copy-start(f32[1,32,16,1440]{3,2,1,0:T(8,128)} %param.16) | copy-start | bytes 8847364
  8.0 2.3 %copy-start.17 = (f32[1,4,16,1440]{3,2,1,0:T(8,128)S(1)}, f32[1,4,16,1440]{3,2,1,0:T(8,128)}, u32[]{:S(2)}) copy-start(f32[1,4,16,1440]{3,2,1,0:T(8,128)} %param.12) | copy-start | bytes 1105924
  8.0 90.1 %reduce-scatter.4.cloned.1.call-start = ((), (), s32[]{:S(2)}) async-start(), calls=%async_computation.2 | async-start | bytes 491520
  10.5 11.2 %collective-permute-start = (f32[3,4,4,1440]{3,2,1,0:T(4,128)S(1)}, f32[3,4,4,1440]{3,2,1,0:T(4,128)S(1)}, u32[]{:S(2)}, u32[]{:S(2)}) collective-permute-start(f32[3,4,4,1440]{3,2,1,0:T(4,128)S(1)} %get-tuple-element.7), channel_id=1, source_target_pairs={{0,2},{2,4},{4,6},{1,3},{3,5},{5,7},{8,10},{10,12},{12,14},{9,11},... | collective-permute-start | bytes 829448 | tf_op jit(solution)/shard_map/ppermute | solution.py:17
  15.4 10.4 %collective-permute-start.1 = (f32[3,4,4,1440]{3,2,1,0:T(4,128)S(1)}, f32[3,4,4,1440]{3,2,1,0:T(4,128)S(1)}, u32[]{:S(2)}, u32[]{:S(2)}) collective-permute-start(f32[3,4,4,1440]{3,2,1,0:T(4,128)S(1)} %get-tuple-element.8), channel_id=1, source_target_pairs={{2,0},{4,2},{6,4},{3,1},{5,3},{7,5},{10,8},{12,10},{14,12},{11,9},... | collective-permute-start | bytes 829448 | tf_op jit(solution)/shard_map/ppermute | solution.py:18
  26.5 6.4 %copy-start.1 = (f32[4,24,1440]{2,1,0:T(8,128)}, f32[4,24,1440]{2,1,0:T(8,128)S(1)}, u32[]{:S(2)}) copy-start(f32[4,24,1440]{2,1,0:T(8,128)S(1)} %get-tuple-element.4) | copy-start | bytes 1658884
  26.5 6.4 %copy-start.3 = (f32[4,24,1440]{2,1,0:T(8,128)}, f32[4,24,1440]{2,1,0:T(8,128)S(1)}, u32[]{:S(2)}) copy-start(f32[4,24,1440]{2,1,0:T(8,128)S(1)} %get-tuple-element.5) | copy-start | bytes 1658884
  26.5 6.4 %copy-start.5 = (f32[4,24,1440]{2,1,0:T(8,128)}, f32[4,24,1440]{2,1,0:T(8,128)S(1)}, u32[]{:S(2)}) copy-start(f32[4,24,1440]{2,1,0:T(8,128)S(1)} %get-tuple-element.6) | copy-start | bytes 1658884
  26.5 6.4 %copy-start.7 = (f32[4,24,1440]{2,1,0:T(8,128)}, f32[4,24,1440]{2,1,0:T(8,128)S(1)}, u32[]{:S(2)}) copy-start(f32[4,24,1440]{2,1,0:T(8,128)S(1)} %get-tuple-element.2) | copy-start | bytes 1658884
  26.5 6.4 %copy-start.9 = (f32[4,24,1440]{2,1,0:T(8,128)}, f32[4,24,1440]{2,1,0:T(8,128)S(1)}, u32[]{:S(2)}) copy-start(f32[4,24,1440]{2,1,0:T(8,128)S(1)} %get-tuple-element.3) | copy-start | bytes 1658884
  33.0 4.7 %copy-start.18 = (s32[1,32]{1,0:T(1,128)S(1)}, s32[1,32]{1,0:T(1,128)}, u32[]{:S(2)}) copy-start(s32[1,32]{1,0:T(1,128)} %param.15) | copy-start | bytes 388
  33.5 10.9 %collective-permute-start.2 = (f32[4,16,1440]{2,1,0:T(8,128)S(1)}, f32[4,16,1440]{2,1,0:T(8,128)}, u32[]{:S(2)}, u32[]{:S(2)}) collective-permute-start(f32[4,16,1440]{2,1,0:T(8,128)S(1)} %fusion.41), channel_id=1, source_target_pairs={{0,8},{8,16},{16,24},{1,9},{9,17},{17,25},{2,10},{10,18},{18,26},{... | collective-permute-start | bytes 1105928 | tf_op jit(solution)/shard_map/ppermute | solution.py:26
  45.6 3.6 %copy-start.16 = (f32[4,16,1440]{2,1,0:T(8,128)}, f32[4,16,1440]{2,1,0:T(8,128)S(1)}, u32[]{:S(2)}) copy-start(f32[4,16,1440]{2,1,0:T(8,128)S(1)} %fusion.46) | copy-start | bytes 1105924
  45.6 3.1 %copy-start.19 = (s32[1,32]{1,0:T(1,128)S(1)}, s32[1,32]{1,0:T(1,128)}, u32[]{:S(2)}) copy-start(s32[1,32]{1,0:T(1,128)} %param.15) | copy-start | bytes 388
  45.6 11.5 %collective-permute-start.3 = (f32[4,16,1440]{2,1,0:T(8,128)S(1)}, f32[4,16,1440]{2,1,0:T(8,128)S(1)}, u32[]{:S(2)}, u32[]{:S(2)}) collective-permute-start(f32[4,16,1440]{2,1,0:T(8,128)S(1)} %fusion.46), channel_id=1, source_target_pairs={{8,0},{16,8},{24,16},{9,1},{17,9},{25,17},{10,2},{18,10},{26,18},{... | collective-permute-start | bytes 1105928 | tf_op jit(solution)/shard_map/ppermute | solution.py:26
  48.7 18.6 %copy-start.2 = (f32[4,24,1440]{2,1,0:T(8,128)S(1)}, f32[4,24,1440]{2,1,0:T(8,128)}, u32[]{:S(2)}) copy-start(f32[4,24,1440]{2,1,0:T(8,128)} %copy-done.1) | copy-start | bytes 1658884
  48.7 18.6 %copy-start.4 = (f32[4,24,1440]{2,1,0:T(8,128)S(1)}, f32[4,24,1440]{2,1,0:T(8,128)}, u32[]{:S(2)}) copy-start(f32[4,24,1440]{2,1,0:T(8,128)} %copy-done.3) | copy-start | bytes 1658884
  57.2 5.7 %collective-permute-start.4 = (f32[1,4,4,1440]{3,2,1,0:T(4,128)S(1)}, f32[1,4,4,1440]{3,2,1,0:T(4,128)S(1)}, u32[]{:S(2)}, u32[]{:S(2)}) collective-permute-start(f32[1,4,4,1440]{3,2,1,0:T(4,128)S(1)} %get-tuple-element.43), channel_id=1, source_target_pairs={{0,2},{2,4},{4,6},{1,3},{3,5},{5,7},{8,10},{10,12},{12,14},{9,11},... | collective-permute-start | bytes 276488 | tf_op jit(solution)/shard_map/ppermute | solution.py:17
  60.7 6.5 %collective-permute-start.5 = (f32[1,4,4,1440]{3,2,1,0:T(4,128)S(1)}, f32[1,4,4,1440]{3,2,1,0:T(4,128)S(1)}, u32[]{:S(2)}, u32[]{:S(2)}) collective-permute-start(f32[1,4,4,1440]{3,2,1,0:T(4,128)S(1)} %get-tuple-element.44), channel_id=1, source_target_pairs={{2,0},{4,2},{6,4},{3,1},{5,3},{7,5},{10,8},{12,10},{14,12},{11,9},... | collective-permute-start | bytes 276488 | tf_op jit(solution)/shard_map/ppermute | solution.py:18
  67.3 1.2 copy-start.8
  67.3 1.4 copy-start.10
  69.2 1.2 copy-start.13
  70.9 1.2 copy-start.15
  73.8 71.9 %all-gather.2.cloned.1.call-start = ((), (), s32[]{:S(2)}) async-start(), calls=%async_computation.1 | async-start | bytes 4718592 | tf_op jit(solution)/shard_map/all_gather | solution.py:121
  (5 other events, 5.1 us)
Sparse Core Ops, SparseCore 0:
  73.9 24.1 reduce-scatter.3
Sparse Core Ops, SparseCore 1:
  75.8 11.4 all-gather.1
where the time goes:
time: 160 us; the launch traced here: 159 us
  blocking collectives  43.4 us (27%)
  waiting for transfers between devices  40.8 us (25%)
  starting transfers between devices  16.9 us (11%)
  between operations  16.6 us (10%)
  other arithmetic  15.9 us (10%)
  matrix products  15 us (9%)
  local copies, waits for them, and re-layouts  10.3 us (6%)
    psum x1, blocking collectives, on_device(): member_coef = lax.psum(local_coef, ('tm', 'lat'))  41 us
    unnamed x3, waiting for transfers between devices  18.7 us
    ppermute x2, waiting for transfers between devices, padded(): after = lax.ppermute(leading, axis, down)  8.45 us
    ppermute x2, starting transfers between devices, padded(): before = lax.ppermute(last, axis, up)  8.45 us
    ppermute x2, waiting for transfers between devices, shifted(): lax.ppermute(value, axis, [(source, source + steps) for source in range(l...  7.97 us
    ppermute x2, waiting for transfers between devices, padded(): before = lax.ppermute(last, axis, up)  5.64 us
    ppermute x2, starting transfers between devices, shifted(): lax.ppermute(value, axis, [(source, source + steps) for source in range(l...  5.58 us
    unnamed x47, local copies, waits for them, and re-layouts  5.51 us
  transfers between devices with their start and end apart: 8, of which 6 were waited for; matrix products, arithmetic and copies ran while one was open for 11% of the time, Pallas kernels for 0%

commit v1 on v0

v1 whole, which is shorter than its diff:
```python
import functools

import jax
import jax.numpy as jnp
from jax import lax
from jax.experimental import pallas as pl
from jax.experimental.pallas import tpu as pltpu
from jax.sharding import PartitionSpec as P

STEPS = 4
MESH = pl.DeviceIdType.MESH
HIGHEST = lax.Precision.HIGHEST
NT = (((1,), (1,)), ((), ()))
NN = (((1,), (0,)), ((), ()))


def mm(a, b, dims, precision=None):
    return lax.dot_general(a, b, dims, precision=precision, preferred_element_type=jnp.float32)


def split(value):
    hi = value.astype(jnp.bfloat16)
    lo = (value - hi.astype(jnp.float32)).astype(jnp.bfloat16)
    return hi, lo


def turn(value, steps, axis):
    return pltpu.roll(value, steps % value.shape[axis], axis)


def extend(ref, where, lon):
    width = ref.shape[-1]
    rem = lon % 128
    last = ref[where + (slice(0, 16), slice(width - 128, width))]
    before = ref[where + (slice(0, 16), slice(width - 256, width - 128))]
    first = ref[where + (slice(0, 16), slice(0, 128))]
    lane = lax.broadcasted_iota(jnp.int32, last.shape, 1)
    wrapped = jnp.where(lane < 128 - rem, turn(before, 128 - rem, 1), turn(last, 128 - rem, 1))
    right = jnp.where(lane < rem + (128 - rem) // 2, turn(first, rem, 1), wrapped)
    ref[where + (slice(0, 16), slice(width - 128, width))] = jnp.where(lane < rem, last, right)


def pack(ref, lead, pair):
    one, two = lead + (2 * pair,), lead + (2 * pair + 1,)
    low = lax.broadcasted_iota(jnp.int32, (8, ref.shape[-1]), 0) < 4
    firsts = jnp.where(low, ref[one + (slice(0, 8),)], turn(ref[two + (slice(0, 8),)], 4, 0))
    lasts = jnp.where(low, turn(ref[one + (slice(8, 16),)], 4, 0), ref[two + (slice(8, 16),)])
    return firsts, lasts


def unpack(ref, lead, pair, after, before):
    low = lax.broadcasted_iota(jnp.int32, (8, ref.shape[-1]), 0) < 4
    ref[lead + (2 * pair, slice(16, 24))] = jnp.where(low, after, turn(before, 4, 0))
    ref[lead + (2 * pair + 1, slice(16, 24))] = jnp.where(low, turn(after, 4, 0), before)


def kernel(
    T, L, E,
    rows_ref, cnt_ref, val_ref, prc_ref, mp_ref, inc_hbm, wlon_hbm, wlat_hbm, jac_hbm, pert_hbm,
    grad_hbm, step_hbm,
    inc_v, wlon_v, wlat_v, jac_v, pert_v, jhi, jlo, wide, coef, adj,
    h_first, h_last, h_after, h_before, a_first, a_last, a_after, a_before,
    end_v, nxt_v, prior_v, forc, rs_v, ca_send, ca_v, cb_send, cb_v, grad_v, step_v,
    load_sem, h_ssem, h_rsem, a_ssem, a_rsem, t_ssem, t_rsem, p_ssem, p_rsem,
    rs_ssem, rs_rsem, ca_ssem, ca_rsem, cb_ssem, cb_rsem, g_ssem, g_rsem, out_sem,
):
    k, b, e = lax.axis_index("tm"), lax.axis_index("lat"), lax.axis_index("ens")
    half, crow, lon = inc_v.shape
    pairs = half // 2
    width = wide.shape[-1]
    members = pert_v.shape[1]
    blocks, slots = val_ref.shape
    flat = blocks * slots
    other = 1 - e
    own = pl.ds(e * half, half)

    loads = [
        pltpu.make_async_copy(inc_hbm.at[own], inc_v, load_sem.at[0]),
        pltpu.make_async_copy(wlon_hbm.at[own], wlon_v, load_sem.at[1]),
        pltpu.make_async_copy(wlat_hbm.at[own], wlat_v, load_sem.at[2]),
        pltpu.make_async_copy(jac_hbm, jac_v, load_sem.at[3]),
        pltpu.make_async_copy(pert_hbm, pert_v.at[e], load_sem.at[4]),
    ]
    for item in loads:
        item.start()

    barrier = pltpu.get_barrier_semaphore()
    group = [(dt, de) for dt in range(T) for de in range(E) if dt or de]

    def mate(dt, de):
        return {"tm": lax.rem(k + dt, T), "ens": lax.rem(e + de, E)}

    for dt, de in group:
        pl.semaphore_signal(barrier, inc=1, device_id=mate(dt, de), device_id_type=MESH)
    for db in range(1, L):
        pl.semaphore_signal(barrier, inc=1, device_id={"lat": lax.rem(b + db, L)}, device_id_type=MESH)

    def remote(src, dst, ssem, rsem, device):
        return pltpu.make_async_remote_copy(
            src_ref=src, dst_ref=dst, send_sem=ssem, recv_sem=rsem, device_id=device, device_id_type=MESH
        )

    up = {"lat": lax.rem(b + 1, L)}
    down = {"lat": lax.rem(b + L - 1, L)}
    later_dev = {"tm": lax.rem(k + 1, T)}
    prior_dev = {"tm": lax.rem(k + T - 1, T)}
    partner = {"ens": other}
    has_up, has_down = b < L - 1, b > 0
    has_later, has_prior = k < T - 1, k > 0

    for item in loads[:3]:
        item.wait()
    for at, ref in enumerate((inc_v, wlon_v, wlat_v)):
        for i in range(half):
            wide[at, i, 0:16, 0:lon] = ref[i]
            extend(wide, (at, i), lon)
        for pair in range(pairs):
            firsts, lasts = pack(wide, (at,), pair)
            h_first[at * pairs + pair] = firsts
            h_last[at * pairs + pair] = lasts

    pl.semaphore_wait(barrier, len(group) + L - 1)

    h_up = remote(h_last, h_before, h_ssem.at[0], h_rsem.at[0], up)
    h_down = remote(h_first, h_after, h_ssem.at[1], h_rsem.at[1], down)
    n_copy = remote(inc_v, nxt_v, t_ssem.at[0], t_rsem.at[0], prior_dev)

    @pl.when(has_up)
    def _():
        h_up.start()

    @pl.when(has_down)
    def _():
        h_down.start()

    @pl.when(has_prior)
    def _():
        n_copy.start()

    loads[4].wait()
    p_copy = remote(pert_v.at[e], pert_v.at[e], p_ssem, p_rsem, partner)
    p_copy.start()

    @pl.when(jnp.logical_not(has_up))
    def _():
        h_after[...] = jnp.zeros_like(h_after)
        a_after[...] = jnp.zeros_like(a_after)

    @pl.when(jnp.logical_not(has_down))
    def _():
        h_before[...] = jnp.zeros_like(h_before)
        a_before[...] = jnp.zeros_like(a_before)

    @pl.when(jnp.logical_not(has_prior))
    def _():
        prior_v[...] = jnp.zeros_like(prior_v)

    loads[3].wait()
    jhi[:, width - 128 : width] = jnp.zeros((flat, 128), jnp.bfloat16)
    jlo[:, width - 128 : width] = jnp.zeros((flat, 128), jnp.bfloat16)

    def cut(at, carry):
        some = pl.ds(pl.multiple_of(at * 32, 32), 32)
        hi, lo = split(jac_v[some, :])
        jhi[some, 0:lon] = hi
        jlo[some, 0:lon] = lo
        return carry

    lax.fori_loop(0, flat // 32, cut, 0)

    column = lax.broadcasted_iota(jnp.int32, (blocks, flat), 1)
    block = lax.broadcasted_iota(jnp.int32, (blocks, flat), 0)
    mine = (column >= block * slots) & (column < (block + 1) * slots)
    spread = mine.astype(jnp.float32)
    first_column = lax.broadcasted_iota(jnp.int32, (1, flat), 1)
    slot = (first_column % slots).astype(jnp.float32)
    tile_slot = lax.broadcasted_iota(jnp.int32, (slots, flat), 0)
    tile_column = lax.broadcasted_iota(jnp.int32, (slots, flat), 1) % slots
    tiled = (tile_slot == tile_column).astype(jnp.float32)

    def flatten(ref):
        return jnp.sum(mm(ref[...], tiled, NN, HIGHEST) * spread, axis=0, keepdims=True)

    values, precisions = flatten(val_ref), flatten(prc_ref)
    counts = mm(jnp.broadcast_to(cnt_ref[...].astype(jnp.float32), (8, blocks)), spread, NN, HIGHEST)[0:1]
    rows = mm(jnp.broadcast_to(rows_ref[...].astype(jnp.float32), (8, blocks)), spread, NN, HIGHEST)[0:1]
    precisions = jnp.where(slot < counts - 0.5, precisions, 0.0)
    local = lax.broadcasted_iota(jnp.int32, (half * crow, flat), 0) + e * (half * crow)
    reads = (jnp.abs(rows - local.astype(jnp.float32)) < 0.5).astype(jnp.float32)

    @pl.when(has_down)
    def _():
        h_up.wait_recv()

    @pl.when(has_up)
    def _():
        h_down.wait_recv()

    for at in range(3):
        for pair in range(pairs):
            slot_at = at * pairs + pair
            unpack(wide, (at,), pair, h_after[slot_at], h_before[slot_at])

    for i in range(half):
        wl, wt = wide[1, i], wide[2, i]
        wl2, wt2 = wl * wl, wt * wt
        coef[i, 0] = 1.0 - wl2 - wt2
        coef[i, 1] = 0.5 * (wl2 - wl)
        coef[i, 2] = 0.5 * (wl2 + wl)
        coef[i, 3] = 0.5 * (wt2 - wt)
        coef[i, 4] = 0.5 * (wt2 + wt)
        for _ in range(STEPS):
            f = wide[0, i]
            wide[0, i] = (
                coef[i, 0] * f
                + coef[i, 1] * turn(f, -1, 1)
                + coef[i, 2] * turn(f, 1, 1)
                + coef[i, 3] * turn(f, -1, 0)
                + coef[i, 4] * turn(f, 1, 0)
            )
        end_v[i] = wide[0, i, 0:crow]

    e_copy = remote(end_v, prior_v, t_ssem.at[1], t_rsem.at[1], later_dev)

    @pl.when(has_later)
    def _():
        e_copy.start()

    fhi, flo = split(jnp.concatenate([end_v[i] for i in range(half)], axis=0))
    jh, jl = jhi[...], jlo[...]
    seen = mm(fhi, jh, NT) + mm(flo, jh, NT) + mm(fhi, jl, NT)
    evolved = jnp.sum(seen * reads, axis=0, keepdims=True)
    whi, wlo = split(reads * (precisions * (evolved - values)))
    placed = mm(whi, jh, NN) + mm(wlo, jh, NN) + mm(whi, jl, NN)

    @pl.when(has_later)
    def _():
        n_copy.wait_recv()

    @pl.when(jnp.logical_not(has_later))
    def _():
        for i in range(half):
            nxt_v[i] = end_v[i, :, 0:lon]

    for i in range(half):
        prec = mp_ref[e * half + i]
        later = prec * (nxt_v[i] - end_v[i, :, 0:lon])
        adj[i, 0:crow, 0:lon] = placed[i * crow : (i + 1) * crow, 0:lon] - later
        extend(adj, (i,), lon)
    for pair in range(pairs):
        firsts, lasts = pack(adj, (), pair)
        a_first[pair] = firsts
        a_last[pair] = lasts
    a_up = remote(a_last, a_before, a_ssem.at[0], a_rsem.at[0], up)
    a_down = remote(a_first, a_after, a_ssem.at[1], a_rsem.at[1], down)

    @pl.when(has_up)
    def _():
        a_up.start()

    @pl.when(has_down)
    def _():
        a_down.start()

    @pl.when(has_down)
    def _():
        a_up.wait_recv()

    @pl.when(has_up)
    def _():
        a_down.wait_recv()

    for pair in range(pairs):
        unpack(adj, (), pair, a_after[pair], a_before[pair])

    def back(i):
        g = adj[i]
        return (
            coef[i, 0] * g
            + turn(coef[i, 1] * g, 1, 1)
            + turn(coef[i, 2] * g, -1, 1)
            + turn(coef[i, 3] * g, 1, 0)
            + turn(coef[i, 4] * g, -1, 0)
        )

    def owner_copy(i, h):
        return remote(
            forc.at[i, h], rs_v.at[k], rs_ssem.at[i, h], rs_rsem.at[k], {"tm": e * half + i, "ens": h}
        )

    for i in range(half):
        for h in range(E):
            forc[i, h] = adj[i, h * 8 : h * 8 + 8]
        for _ in range(STEPS - 1):
            adj[i] = back(i)
            for h in range(E):
                forc[i, h] += adj[i, h * 8 : h * 8 + 8]
        for h in range(E):
            here = (k == e * half + i) & (e == h)

            @pl.when(here)
            def _():
                rs_v[k] = forc[i, h]

            @pl.when(jnp.logical_not(here))
            def _():
                owner_copy(i, h).start()

    @pl.when(has_prior)
    def _():
        e_copy.wait_recv()

    for i in range(half):
        prec = mp_ref[e * half + i]
        g = back(i)
        grad_v[e * half + i] = g[0:crow, 0:lon] + prec * (inc_v[i] - prior_v[i, :, 0:lon])
    g_copy = remote(grad_v.at[own], grad_v.at[own], g_ssem, g_rsem, partner)
    g_copy.start()

    p_copy.wait_recv()
    for at in range(T):
        inside = (k == at) & (e == at // half)

        @pl.when(jnp.logical_not(inside))
        def _():
            remote(forc.at[0, 0], rs_v.at[at], rs_ssem.at[0, 0], rs_rsem.at[at], partner).wait_recv()

    total = rs_v[0]
    for at in range(1, T):
        total = total + rs_v[at]
    total = total[:, 0:lon]
    lane = lax.broadcasted_iota(jnp.int32, (8, 128), 1)
    part = jnp.zeros((8, 128), jnp.float32)
    for m in range(E * members):
        dots = jnp.sum(pert_v[m // members, m % members, e] * total, axis=1, keepdims=True)
        part = jnp.where(lane == m, dots, part)
    ca_send[...] = part
    me = k * E + e
    ca_v[me] = part
    ca_copies = []
    for dt, de in group:
        copy = remote(ca_send, ca_v.at[me], ca_ssem.at[dt * E + de], ca_rsem.at[me], mate(dt, de))
        copy.start()
        ca_copies.append(copy)
    for dt, de in group:
        it = lax.rem(k + dt, T) * E + lax.rem(e + de, E)
        remote(ca_send, ca_v.at[it], ca_ssem.at[0], ca_rsem.at[it], partner).wait_recv()
    part = ca_v[0]
    for at in range(1, T * E):
        part = part + ca_v[at]
    cb_send[...] = part
    cb_v[b] = part
    cb_copies = []
    for db in range(1, L):
        copy = remote(cb_send, cb_v.at[b], cb_ssem.at[db], cb_rsem.at[b], {"lat": lax.rem(b + db, L)})
        copy.start()
        cb_copies.append(copy)

    g_copy.wait_recv()
    g_out = pltpu.make_async_copy(grad_v, grad_hbm, out_sem.at[0])
    g_out.start()

    for db in range(1, L):
        it = lax.rem(b + db, L)
        remote(cb_send, cb_v.at[it], cb_ssem.at[0], cb_rsem.at[it], partner).wait_recv()
    part = cb_v[0]
    for at in range(1, L):
        part = part + cb_v[at]
    factor = jnp.broadcast_to(jnp.sum(part, axis=0, keepdims=True), (8, 128)) * (-1.0 / (E * members - 1.0))
    for h in range(crow // 8):
        mixed = jnp.zeros((8, lon), jnp.float32)
        for m in range(E * members):
            mixed = mixed + factor[:, m : m + 1] * pert_v[m // members, m % members, h]
        step_v[h * 8 : h * 8 + 8, :] = mixed
    s_out = pltpu.make_async_copy(step_v, step_hbm, out_sem.at[1])
    s_out.start()

    @pl.when(has_up)
    def _():
        h_up.wait_send()
        a_up.wait_send()

    @pl.when(has_down)
    def _():
        h_down.wait_send()
        a_down.wait_send()

    @pl.when(has_prior)
    def _():
        n_copy.wait_send()

    @pl.when(has_later)
    def _():
        e_copy.wait_send()

    p_copy.wait_send()
    g_copy.wait_send()
    for i in range(half):
        for h in range(E):
            here = (k == e * half + i) & (e == h)

            @pl.when(jnp.logical_not(here))
            def _():
                owner_copy(i, h).wait_send()

    for copy in ca_copies + cb_copies:
        copy.wait_send()
    g_out.wait()
    s_out.wait()


def on_device(T, L, E, increment, wind_lon, wind_lat, model_precision, perturbations, obs_rows, obs_jacobian,
              obs_values, obs_precision, obs_counts):
    _, levels, crow, lon = increment.shape
    members = perturbations.shape[0]
    blocks, slots = obs_jacobian.shape[1:3]
    half, width = levels // E, -(-lon // 128) * 128
    pairs, flat = half // 2, blocks * slots
    f32, dma = jnp.float32, pltpu.SemaphoreType.DMA
    vmem, anyw = pl.BlockSpec(memory_space=pltpu.VMEM), pl.BlockSpec(memory_space=pl.ANY)

    def buf(*shape, kind=f32):
        return pltpu.VMEM(shape, kind)

    grad, step = pl.pallas_call(
        functools.partial(kernel, T, L, E),
        out_shape=(
            jax.ShapeDtypeStruct((levels, crow, lon), f32),
            jax.ShapeDtypeStruct((crow, lon), f32),
        ),
        in_specs=[vmem] * 4 + [pl.BlockSpec(memory_space=pltpu.SMEM)] + [anyw] * 5,
        out_specs=(anyw, anyw),
        scratch_shapes=[
            buf(half, crow, lon), buf(half, crow, lon), buf(half, crow, lon),
            buf(flat, lon), buf(E, members, crow // 8, 8, lon),
            buf(flat, width, kind=jnp.bfloat16), buf(flat, width, kind=jnp.bfloat16),
            buf(3, half, 24, width), buf(half, 5, 24, width), buf(half, 24, width),
            buf(3 * pairs, 8, width), buf(3 * pairs, 8, width), buf(3 * pairs, 8, width), buf(3 * pairs, 8, width),
            buf(pairs, 8, width), buf(pairs, 8, width), buf(pairs, 8, width), buf(pairs, 8, width),
            buf(half, crow, width), buf(half, crow, lon), buf(half, crow, width),
            buf(half, E, 8, width), buf(T, 8, width),
            buf(8, 128), buf(T * E, 8, 128), buf(8, 128), buf(L, 8, 128),
            buf(levels, crow, lon), buf(crow, lon),
            dma((5,)), dma((2,)), dma((2,)), dma((2,)), dma((2,)), dma((2,)), dma((2,)), dma, dma,
            dma((half, E)), dma((T,)), dma((T * E,)), dma((T * E,)), dma((L,)), dma((L,)), dma, dma, dma((2,)),
        ],
        compiler_params=pltpu.CompilerParams(
            collective_id=0, has_side_effects=True, vmem_limit_bytes=60 * 1024 * 1024
        ),
    )(
        obs_rows, obs_counts, obs_values[0], obs_precision[0], model_precision,
        increment[0], wind_lon[0], wind_lat[0],
        obs_jacobian.reshape(flat, lon),
        perturbations.reshape(members, crow // 8, 8, lon),
    )
    return grad[None], step[None]


def solution(mesh):
    T, L, E = mesh.shape["tm"], mesh.shape["lat"], mesh.shape["ens"]
    placed = (
        P("tm", None, "lat", None),
        P("tm", None, "lat", None),
        P("tm", None, "lat", None),
        P(),
        P("ens", "tm", "lat", None),
        P("tm", "lat"),
        P("tm", "lat", None, None),
        P("tm", "lat", None),
        P("tm", "lat", None),
        P("tm", "lat"),
    )
    return jax.shard_map(
        functools.partial(on_device, T, L, E),
        mesh=mesh,
        in_specs=placed,
        out_specs=(P("tm", None, "lat", None), P("tm", "lat", None)),
        check_vma=False,
    )
```

time: 160 us -> 37.4 us (0.23)
  blocking collectives: 43.4 us -> 0 us
  waiting for transfers between devices: 40.8 us -> 0 us
  Pallas kernels: 0 us -> 30.4 us
  starting transfers between devices: 16.9 us -> 0 us
  between operations: 16.6 us -> 0.64 us
  other arithmetic: 15.9 us -> 0 us
  matrix products: 15 us -> 0 us
  local copies, waits for them, and re-layouts: 10.3 us -> 6.06 us
    psum x1 -> x0, blocking collectives: 41 us -> none  [on_device(): member_coef = lax.psum(local_coef, ('tm', 'lat'))]
    pallas_call x0 -> x1, Pallas kernels: none -> 30.4 us  [on_device(): pl.pallas_call(functools.partial(kernel, T, L, E), out_shape=(jax.ShapeDt...]
    ppermute x6 -> x0, waiting for transfers between devices: 22.1 us -> none  [the longest x2 8.45 us: padded(): after = lax.ppermute(leading, axis, down)]
    unnamed x3 -> x0, waiting for transfers between devices: 18.7 us -> none
    ppermute x6 -> x0, starting transfers between devices: 16.8 us -> none  [the longest x2 8.45 us: padded(): before = lax.ppermute(last, axis, up)]
    dot_general x6 -> x0, matrix products: 15 us -> none  [the longest x1 5.08 us: on_device(): jnp.einsum('m,mlan->lan', every_coef, every_member, precision=highest)]
    slice x3 -> x0, other arithmetic: 5.09 us -> none  [trim_coefs(): return tuple((item[:, first:last] for item in coefs))]
    mul x6 -> x0, other arithmetic: 3.48 us -> none  [the longest x1 1.33 us: on_device(): weighted = obs_precision[0] * (evolved - obs_values[0]) * used]
  transfers between devices with their start and end apart: 8 -> 0, of which waited for: 6 -> 0; matrix products, arithmetic and copies ran while one was open for 11% -> 0% of each run, Pallas kernels for 0% -> 0%
where the time goes in v1:
time: 37.4 us; the launch traced here: 37.1 us
  Pallas kernels  30.4 us (81%)
  local copies, waits for them, and re-layouts  6.06 us (16%)
  between operations  0.64 us (2%)
    pallas_call x1, Pallas kernels, on_device(): pl.pallas_call(functools.partial(kernel, T, L, E), out_shape=(jax.ShapeDt...  30.4 us
    unnamed x4, local copies, waits for them, and re-layouts  6.06 us

profile of v1, /device:TPU:0, one launch (start us, length us, event | category | flops | bytes accessed | tf_op | source)
XLA Modules:
  0.0 37.1 jit_solution(15413953517532708443)
XLA Ops:
  0.6 1.4 %copy.12 = f32[1,32,16]{2,1,0:T(8,128)} copy(f32[1,32,16]{1,2,0:T(8,128)} %param.17) | data formatting | bytes 4096 | tf_op args[7]
  2.0 1.4 %copy.13 = f32[1,32,16]{2,1,0:T(8,128)} copy(f32[1,32,16]{1,2,0:T(8,128)} %param.18) | data formatting | bytes 4096 | tf_op args[8]
  3.4 30.4 %shard_map.113 = (f32[4,16,1440]{2,1,0:T(8,128)}, f32[16,1440]{1,0:T(8,128)}) custom-call(s32[1,32]{1,0:T(1,128)} %rows_ref.1, s32[1,32]{1,0:T(1,128)} %cnt_ref.1, f32[32,16]{1,0:T(8,128)} %bitcast.16, f32[32,16]{1,0:T(8,128)} %bitcast.17, f32[4]{0:T(128)} %mp_ref.1, f32[4,16,1440]{2,1,0:T(8,128)} %bitcast.11, f32[4,16,1440]{2,1,0:T(8,128)} %bitcast.12, ...), custom_call_target="tpu_custom_call" | custom-call | tf_op jit(solution)/shard_map/pallas_call | solution.py:425
  33.8 1.8 %copy.16 = f32[1,4,16,1440]{3,2,1,0:T(8,128)} copy(f32[1,4,16,1440]{3,2,1,0:T(8,128)} %bitcast.14) | data formatting | bytes 737280
  35.5 1.5 %copy.17 = f32[1,16,1440]{2,1,0:T(8,128)} copy(f32[1,16,1440]{2,1,0:T(8,128)} %bitcast.15) | data formatting | bytes 184320

commit v2 on v1

--- a/solution.py
+++ b/solution.py
@@ -56,20 +56,20 @@
 
 def kernel(
     T, L, E,
-    rows_ref, cnt_ref, val_ref, prc_ref, mp_ref, inc_hbm, wlon_hbm, wlat_hbm, jac_hbm, pert_hbm,
-    grad_hbm, step_hbm,
-    inc_v, wlon_v, wlat_v, jac_v, pert_v, jhi, jlo, wide, coef, adj,
-    h_first, h_last, h_after, h_before, a_first, a_last, a_after, a_before,
-    end_v, nxt_v, prior_v, forc, rs_v, ca_send, ca_v, cb_send, cb_v, grad_v, step_v,
+    rows_hbm, cnt_hbm, val_hbm, prc_hbm, mp_hbm, inc_hbm, wlon_hbm, wlat_hbm, jac_hbm, pert_hbm,
+    grad_v, pert_v, cb_v,
+    rows_ref, cnt_ref, val_ref, prc_ref, mp_ref, inc_v, wlon_v, wlat_v, jac_v, jhi, jlo, wide, coef, adj,
+    h_first, h_last, h_after, h_before, a_up_v, a_down_v, a_after, a_before,
+    end_v, nxt_v, prior_v, forc, edge, rs_v, edge_v, ca_send, ca_v, cb_send,
     load_sem, h_ssem, h_rsem, a_ssem, a_rsem, t_ssem, t_rsem, p_ssem, p_rsem,
-    rs_ssem, rs_rsem, ca_ssem, ca_rsem, cb_ssem, cb_rsem, g_ssem, g_rsem, out_sem,
+    rs_ssem, rs_rsem, ed_ssem, ed_rsem, ca_ssem, ca_rsem, cb_ssem, cb_rsem, g_ssem, g_rsem,
 ):
     k, b, e = lax.axis_index("tm"), lax.axis_index("lat"), lax.axis_index("ens")
     half, crow, lon = inc_v.shape
     pairs = half // 2
     width = wide.shape[-1]
     members = pert_v.shape[1]
-    blocks, slots = val_ref.shape
+    slots, blocks = val_ref.shape
     flat = blocks * slots
     other = 1 - e
     own = pl.ds(e * half, half)
@@ -80,6 +80,11 @@
         pltpu.make_async_copy(wlat_hbm.at[own], wlat_v, load_sem.at[2]),
         pltpu.make_async_copy(jac_hbm, jac_v, load_sem.at[3]),
         pltpu.make_async_copy(pert_hbm, pert_v.at[e], load_sem.at[4]),
+        pltpu.make_async_copy(rows_hbm, rows_ref, load_sem.at[5]),
+        pltpu.make_async_copy(cnt_hbm, cnt_ref, load_sem.at[6]),
+        pltpu.make_async_copy(val_hbm, val_ref, load_sem.at[7]),
+        pltpu.make_async_copy(prc_hbm, prc_ref, load_sem.at[8]),
+        pltpu.make_async_copy(mp_hbm, mp_ref, load_sem.at[9]),
     ]
     for item in loads:
         item.start()
@@ -155,6 +160,14 @@
     def _():
         prior_v[...] = jnp.zeros_like(prior_v)
 
+    edge_in = ((e == 0) & has_down) | ((e == E - 1) & has_up)
+
+    @pl.when(jnp.logical_not(edge_in))
+    def _():
+        edge_v[...] = jnp.zeros_like(edge_v)
+
+    for item in loads[5:]:
+        item.wait()
     loads[3].wait()
     jhi[:, width - 128 : width] = jnp.zeros((flat, 128), jnp.bfloat16)
     jlo[:, width - 128 : width] = jnp.zeros((flat, 128), jnp.bfloat16)
@@ -179,7 +192,7 @@
     tiled = (tile_slot == tile_column).astype(jnp.float32)
 
     def flatten(ref):
-        return jnp.sum(mm(ref[...], tiled, NN, HIGHEST) * spread, axis=0, keepdims=True)
+        return jnp.sum(mm(ref[...], spread, NN, HIGHEST) * tiled, axis=0, keepdims=True)
 
     values, precisions = flatten(val_ref), flatten(prc_ref)
     counts = mm(jnp.broadcast_to(cnt_ref[...].astype(jnp.float32), (8, blocks)), spread, NN, HIGHEST)[0:1]
@@ -247,31 +260,7 @@
         later = prec * (nxt_v[i] - end_v[i, :, 0:lon])
         adj[i, 0:crow, 0:lon] = placed[i * crow : (i + 1) * crow, 0:lon] - later
         extend(adj, (i,), lon)
-    for pair in range(pairs):
-        firsts, lasts = pack(adj, (), pair)
-        a_first[pair] = firsts
-        a_last[pair] = lasts
-    a_up = remote(a_last, a_before, a_ssem.at[0], a_rsem.at[0], up)
-    a_down = remote(a_first, a_after, a_ssem.at[1], a_rsem.at[1], down)
-
-    @pl.when(has_up)
-    def _():
-        a_up.start()
-
-    @pl.when(has_down)
-    def _():
-        a_down.start()
-
-    @pl.when(has_down)
-    def _():
-        a_up.wait_recv()
-
-    @pl.when(has_up)
-    def _():
-        a_down.wait_recv()
-
-    for pair in range(pairs):
-        unpack(adj, (), pair, a_after[pair], a_before[pair])
+        adj[i, crow : crow + 8] = jnp.zeros((8, width), jnp.float32)
 
     def back(i):
         g = adj[i]
@@ -288,13 +277,34 @@
             forc.at[i, h], rs_v.at[k], rs_ssem.at[i, h], rs_rsem.at[k], {"tm": e * half + i, "ens": h}
         )
 
+    def edge_copy(i, h, device):
+        return remote(edge.at[i, h], edge_v.at[k], ed_ssem.at[i, h], ed_rsem.at[k], device)
+
+    edge_up = [edge_copy(i, 0, {"tm": e * half + i, "lat": lax.rem(b + 1, L), "ens": 0}) for i in range(half)]
+    edge_down = [
+        edge_copy(i, 1, {"tm": e * half + i, "lat": lax.rem(b + L - 1, L), "ens": E - 1}) for i in range(half)
+    ]
+
     for i in range(half):
         for h in range(E):
             forc[i, h] = adj[i, h * 8 : h * 8 + 8]
+        rim = jnp.zeros((8, width), jnp.float32)
         for _ in range(STEPS - 1):
             adj[i] = back(i)
             for h in range(E):
                 forc[i, h] += adj[i, h * 8 : h * 8 + 8]
+            rim = rim + adj[i, crow : crow + 8]
+        edge[i, 0] = rim[0:4]
+        edge[i, 1] = rim[4:8]
+
+        @pl.when(has_up)
+        def _():
+            edge_up[i].start()
+
+        @pl.when(has_down)
+        def _():
+            edge_down[i].start()
+
         for h in range(E):
             here = (k == e * half + i) & (e == h)
 
@@ -306,14 +316,38 @@
             def _():
                 owner_copy(i, h).start()
 
+    for i in range(half):
+        adj[i] = back(i)
+        a_up_v[i] = adj[i, crow : crow + 4]
+        a_down_v[i] = adj[i, crow + 4 : crow + 8]
+    a_up = remote(a_up_v, a_before, a_ssem.at[0], a_rsem.at[0], up)
+    a_down = remote(a_down_v, a_after, a_ssem.at[1], a_rsem.at[1], down)
+
+    @pl.when(has_up)
+    def _():
+        a_up.start()
+
+    @pl.when(has_down)
+    def _():
+        a_down.start()
+
     @pl.when(has_prior)
     def _():
         e_copy.wait_recv()
 
+    @pl.when(has_down)
+    def _():
+        a_up.wait_recv()
+
+    @pl.when(has_up)
+    def _():
+        a_down.wait_recv()
+
     for i in range(half):
         prec = mp_ref[e * half + i]
-        g = back(i)
-        grad_v[e * half + i] = g[0:crow, 0:lon] + prec * (inc_v[i] - prior_v[i, :, 0:lon])
+        gap = jnp.zeros((crow - 8, lon), jnp.float32)
+        rims = jnp.concatenate([a_before[i][:, 0:lon], gap, a_after[i][:, 0:lon]], axis=0)
+        grad_v[e * half + i] = adj[i, 0:crow, 0:lon] + rims + prec * (inc_v[i] - prior_v[i, :, 0:lon])
     g_copy = remote(grad_v.at[own], grad_v.at[own], g_ssem, g_rsem, partner)
     g_copy.start()
 
@@ -325,9 +359,18 @@
         def _():
             remote(forc.at[0, 0], rs_v.at[at], rs_ssem.at[0, 0], rs_rsem.at[at], partner).wait_recv()
 
-    total = rs_v[0]
+    @pl.when(edge_in)
+    def _():
+        for at in range(T):
+            remote(edge.at[0, 0], edge_v.at[at], ed_ssem.at[0, 0], ed_rsem.at[at], partner).wait_recv()
+
+    total, rim = rs_v[0], edge_v[0]
     for at in range(1, T):
         total = total + rs_v[at]
+        rim = rim + edge_v[at]
+    line = lax.broadcasted_iota(jnp.int32, (8, width), 0)
+    rim = jnp.concatenate([rim, rim], axis=0)
+    total = total + jnp.where((line < 4) == (e == 0), rim, 0.0)
     total = total[:, 0:lon]
     lane = lax.broadcasted_iota(jnp.int32, (8, 128), 1)
     part = jnp.zeros((8, 128), jnp.float32)
@@ -357,54 +400,66 @@
         cb_copies.append(copy)
 
     g_copy.wait_recv()
-    g_out = pltpu.make_async_copy(grad_v, grad_hbm, out_sem.at[0])
-    g_out.start()
-
     for db in range(1, L):
         it = lax.rem(b + db, L)
         remote(cb_send, cb_v.at[it], cb_ssem.at[0], cb_rsem.at[it], partner).wait_recv()
+    @pl.when(has_up)
+    def _():
+        h_up.wait_send()
+        a_up.wait_send()
+
+    @pl.when(has_down)
+    def _():
+        h_down.wait_send()
+        a_down.wait_send()
+
+    @pl.when(has_prior)
+    def _():
+        n_copy.wait_send()
+
+    @pl.when(has_later)
+    def _():
+        e_copy.wait_send()
+
+    p_copy.wait_send()
+    g_copy.wait_send()
+    for i in range(half):
+        for h in range(E):
+            here = (k == e * half + i) & (e == h)
+
+            @pl.when(jnp.logical_not(here))
+            def _():
+                owner_copy(i, h).wait_send()
+
+    for i in range(half):
+        @pl.when(has_up)
+        def _():
+            edge_up[i].wait_send()
+
+        @pl.when(has_down)
+        def _():
+            edge_down[i].wait_send()
+
+    for copy in ca_copies + cb_copies:
+        copy.wait_send()
+
+
+def finish(L, grad_v, pert_v, cb_v, grad_hbm, step_hbm, step_v, out_sem):
+    g_out = pltpu.make_async_copy(grad_v, grad_hbm, out_sem.at[0])
+    g_out.start()
+    ens, members, rows, _, lon = pert_v.shape
+    count = ens * members
     part = cb_v[0]
     for at in range(1, L):
         part = part + cb_v[at]
-    factor = jnp.broadcast_to(jnp.sum(part, axis=0, keepdims=True), (8, 128)) * (-1.0 / (E * members - 1.0))
-    for h in range(crow // 8):
+    factor = jnp.broadcast_to(jnp.sum(part, axis=0, keepdims=True), (8, 128)) * (-1.0 / (count - 1.0))
+    for h in range(rows):
         mixed = jnp.zeros((8, lon), jnp.float32)
-        for m in range(E * members):
+        for m in range(count):
             mixed = mixed + factor[:, m : m + 1] * pert_v[m // members, m % members, h]
         step_v[h * 8 : h * 8 + 8, :] = mixed
     s_out = pltpu.make_async_copy(step_v, step_hbm, out_sem.at[1])
     s_out.start()
-
-    @pl.when(has_up)
-    def _():
-        h_up.wait_send()
-        a_up.wait_send()
-
-    @pl.when(has_down)
-    def _():
-        h_down.wait_send()
-        a_down.wait_send()
-
-    @pl.when(has_prior)
-    def _():
-        n_copy.wait_send()
-
-    @pl.when(has_later)
-    def _():
-        e_copy.wait_send()
-
-    p_copy.wait_send()
-    g_copy.wait_send()
-    for i in range(half):
-        for h in range(E):
-            here = (k == e * half + i) & (e == h)
-
-            @pl.when(jnp.logical_not(here))
-            def _():
-                owner_copy(i, h).wait_send()
-
-    for copy in ca_copies + cb_copies:
-        copy.wait_send()
     g_out.wait()
     s_out.wait()
 
@@ -422,37 +477,51 @@
     def buf(*shape, kind=f32):
         return pltpu.VMEM(shape, kind)
 
+    parts = pl.pallas_call(
+        functools.partial(kernel, T, L, E),
+        out_shape=(
+            buf(levels, crow, lon),
+            buf(E, members, crow // 8, 8, lon),
+            buf(L, 8, 128),
+        ),
+        in_specs=[pl.BlockSpec(memory_space=pltpu.HBM)] * 10,
+        out_specs=(vmem, vmem, vmem),
+        scratch_shapes=[
+            pltpu.VMEM((1, blocks), jnp.int32), pltpu.VMEM((1, blocks), jnp.int32),
+            buf(slots, blocks), buf(slots, blocks), pltpu.SMEM((levels,), f32),
+            buf(half, crow, lon), buf(half, crow, lon), buf(half, crow, lon),
+            buf(flat, lon),
+            buf(flat, width, kind=jnp.bfloat16), buf(flat, width, kind=jnp.bfloat16),
+            buf(3, half, 24, width), buf(half, 5, 24, width), buf(half, 24, width),
+            buf(3 * pairs, 8, width), buf(3 * pairs, 8, width), buf(3 * pairs, 8, width), buf(3 * pairs, 8, width),
+            buf(half, 4, width), buf(half, 4, width), buf(half, 4, width), buf(half, 4, width),
+            buf(half, crow, width), buf(half, crow, lon), buf(half, crow, width),
+            buf(half, E, 8, width), buf(half, 2, 4, width), buf(T, 8, width), buf(T, 4, width),
+            buf(8, 128), buf(T * E, 8, 128), buf(8, 128),
+            dma((10,)), dma((2,)), dma((2,)), dma((2,)), dma((2,)), dma((2,)), dma((2,)), dma, dma,
+            dma((half, E)), dma((T,)), dma((half, 2)), dma((T,)),
+            dma((T * E,)), dma((T * E,)), dma((L,)), dma((L,)), dma, dma,
+        ],
+        compiler_params=pltpu.CompilerParams(
+            collective_id=0, has_side_effects=True, vmem_limit_bytes=56 * 1024 * 1024
+        ),
+    )(
+        obs_rows, obs_counts, obs_values[0].T, obs_precision[0].T, model_precision,
+        increment[0], wind_lon[0], wind_lat[0],
+        obs_jacobian.reshape(flat, lon),
+        perturbations.reshape(members, crow // 8, 8, lon),
+    )
     grad, step = pl.pallas_call(
-        functools.partial(kernel, T, L, E),
+        functools.partial(finish, L),
         out_shape=(
             jax.ShapeDtypeStruct((levels, crow, lon), f32),
             jax.ShapeDtypeStruct((crow, lon), f32),
         ),
-        in_specs=[vmem] * 4 + [pl.BlockSpec(memory_space=pltpu.SMEM)] + [anyw] * 5,
+        in_specs=[vmem] * 3,
         out_specs=(anyw, anyw),
-        scratch_shapes=[
-            buf(half, crow, lon), buf(half, crow, lon), buf(half, crow, lon),
-            buf(flat, lon), buf(E, members, crow // 8, 8, lon),
-            buf(flat, width, kind=jnp.bfloat16), buf(flat, width, kind=jnp.bfloat16),
-            buf(3, half, 24, width), buf(half, 5, 24, width), buf(half, 24, width),
-            buf(3 * pairs, 8, width), buf(3 * pairs, 8, width), buf(3 * pairs, 8, width), buf(3 * pairs, 8, width),
-            buf(pairs, 8, width), buf(pairs, 8, width), buf(pairs, 8, width), buf(pairs, 8, width),
-            buf(half, crow, width), buf(half, crow, lon), buf(half, crow, width),
-            buf(half, E, 8, width), buf(T, 8, width),
-            buf(8, 128), buf(T * E, 8, 128), buf(8, 128), buf(L, 8, 128),
-            buf(levels, crow, lon), buf(crow, lon),
-            dma((5,)), dma((2,)), dma((2,)), dma((2,)), dma((2,)), dma((2,)), dma((2,)), dma, dma,
-            dma((half, E)), dma((T,)), dma((T * E,)), dma((T * E,)), dma((L,)), dma((L,)), dma, dma, dma((2,)),
-        ],
-        compiler_params=pltpu.CompilerParams(
-            collective_id=0, has_side_effects=True, vmem_limit_bytes=60 * 1024 * 1024
-        ),
-    )(
-        obs_rows, obs_counts, obs_values[0], obs_precision[0], model_precision,
-        increment[0], wind_lon[0], wind_lat[0],
-        obs_jacobian.reshape(flat, lon),
-        perturbations.reshape(members, crow // 8, 8, lon),
-    )
+        scratch_shapes=[buf(crow, lon), dma((2,))],
+        compiler_params=pltpu.CompilerParams(vmem_limit_bytes=8 * 1024 * 1024),
+    )(*[pltpu.with_memory_space_constraint(item, pltpu.VMEM) for item in parts])
     return grad[None], step[None]
 
 

time: 37.4 us -> 28.3 us (0.76)
  local copies, waits for them, and re-layouts: 6.06 us -> 0 us
  Pallas kernels: 30.4 us -> 27.5 us
    unnamed x4 -> x0, local copies, waits for them, and re-layouts: 6.06 us -> none
    pallas_call x1 -> x2, Pallas kernels: 30.4 us -> 27.5 us  [the longest x1 26.6 us: on_device(): pl.pallas_call(functools.partial(kernel, T, L, E), out_shape=(buf(levels,...]
where the time goes in v2:
time: 28.3 us; the launch traced here: 28.2 us
  Pallas kernels  27.5 us (97%)
  between operations  0.64 us (2%)
    pallas_call x1, Pallas kernels, on_device(): pl.pallas_call(functools.partial(kernel, T, L, E), out_shape=(buf(levels,...  26.6 us
    pallas_call x1, Pallas kernels, on_device(): pl.pallas_call(functools.partial(finish, L), out_shape=(jax.ShapeDtypeStr...  0.94 us

profile of v2, /device:TPU:0, one launch (start us, length us, event | category | flops | bytes accessed | tf_op | source)
XLA Modules:
  0.0 28.2 jit_solution(9843403966769144826)
XLA Ops:
  0.6 26.6 %shard_map.113 = (f32[4,16,1440]{2,1,0:T(8,128)S(1)}, f32[2,16,2,8,1440]{4,3,2,1,0:T(8,128)S(1)}, f32[4,8,128]{2,1,0:T(8,128)S(1)}) custom-call(s32[1,32]{1,0:T(1,128)} %rows_hbm.1, s32[1,32]{1,0:T(1,128)} %cnt_hbm.1, f32[16,32]{1,0:T(8,128)} %bitcast.18, f32[16,32]{1,0:T(8,128)} %bitcast.19, f32[4]{0:T(128)} %mp_hbm.1, f32[4,16,1440]{2,1,0:T(8,128)} %bitcast.15, ...), custom_call_target="tpu_custom_call" | custom-call | tf_op jit(solution)/shard_map/pallas_call | solution.py:480
  27.2 0.9 %shard_map.114 = (f32[4,16,1440]{2,1,0:T(8,128)}, f32[16,1440]{1,0:T(8,128)}) custom-call(f32[4,16,1440]{2,1,0:T(8,128)S(1)} %get-tuple-element.7.grad_v, f32[2,16,2,8,1440]{4,3,2,1,0:T(8,128)S(1)} %get-tuple-element.8.pert_v, f32[4,8,128]{2,1,0:T(8,128)S(1)} %get-tuple-element.9.cb_v), custom_call_target="tpu_custom_call" | custom-call | tf_op jit(solution)/shard_map/pallas_call | solution.py:514

commit v3 on v2

--- a/solution.py
+++ b/solution.py
@@ -40,20 +40,6 @@
     ref[where + (slice(0, 16), slice(width - 128, width))] = jnp.where(lane < rem, last, right)
 
 
-def pack(ref, lead, pair):
-    one, two = lead + (2 * pair,), lead + (2 * pair + 1,)
-    low = lax.broadcasted_iota(jnp.int32, (8, ref.shape[-1]), 0) < 4
-    firsts = jnp.where(low, ref[one + (slice(0, 8),)], turn(ref[two + (slice(0, 8),)], 4, 0))
-    lasts = jnp.where(low, turn(ref[one + (slice(8, 16),)], 4, 0), ref[two + (slice(8, 16),)])
-    return firsts, lasts
-
-
-def unpack(ref, lead, pair, after, before):
-    low = lax.broadcasted_iota(jnp.int32, (8, ref.shape[-1]), 0) < 4
-    ref[lead + (2 * pair, slice(16, 24))] = jnp.where(low, after, turn(before, 4, 0))
-    ref[lead + (2 * pair + 1, slice(16, 24))] = jnp.where(low, turn(after, 4, 0), before)
-
-
 def kernel(
     T, L, E,
     rows_hbm, cnt_hbm, val_hbm, prc_hbm, mp_hbm, inc_hbm, wlon_hbm, wlat_hbm, jac_hbm, pert_hbm,
@@ -61,12 +47,11 @@
     rows_ref, cnt_ref, val_ref, prc_ref, mp_ref, inc_v, wlon_v, wlat_v, jac_v, jhi, jlo, wide, coef, adj,
     h_first, h_last, h_after, h_before, a_up_v, a_down_v, a_after, a_before,
     end_v, nxt_v, prior_v, forc, edge, rs_v, edge_v, ca_send, ca_v, cb_send,
-    load_sem, h_ssem, h_rsem, a_ssem, a_rsem, t_ssem, t_rsem, p_ssem, p_rsem,
+    load_sem, h_ssem, h_rsem, a_ssem, a_rsem, t_ssem, t_rsem, e_ssem, e_rsem, p_ssem, p_rsem,
     rs_ssem, rs_rsem, ed_ssem, ed_rsem, ca_ssem, ca_rsem, cb_ssem, cb_rsem, g_ssem, g_rsem,
 ):
     k, b, e = lax.axis_index("tm"), lax.axis_index("lat"), lax.axis_index("ens")
     half, crow, lon = inc_v.shape
-    pairs = half // 2
     width = wide.shape[-1]
     members = pert_v.shape[1]
     slots, blocks = val_ref.shape
@@ -119,24 +104,24 @@
         for i in range(half):
             wide[at, i, 0:16, 0:lon] = ref[i]
             extend(wide, (at, i), lon)
-        for pair in range(pairs):
-            firsts, lasts = pack(wide, (at,), pair)
-            h_first[at * pairs + pair] = firsts
-            h_last[at * pairs + pair] = lasts
+            h_first[i, at] = wide[at, i, 0:4]
+            h_last[i, at] = wide[at, i, crow - 4 : crow]
 
     pl.semaphore_wait(barrier, len(group) + L - 1)
 
-    h_up = remote(h_last, h_before, h_ssem.at[0], h_rsem.at[0], up)
-    h_down = remote(h_first, h_after, h_ssem.at[1], h_rsem.at[1], down)
+    h_up = [remote(h_last.at[i], h_before.at[i], h_ssem.at[0, i], h_rsem.at[0, i], up) for i in range(half)]
+    h_down = [remote(h_first.at[i], h_after.at[i], h_ssem.at[1, i], h_rsem.at[1, i], down) for i in range(half)]
+    e_copy = [remote(end_v.at[i], prior_v.at[i], e_ssem.at[i], e_rsem.at[i], later_dev) for i in range(half)]
     n_copy = remote(inc_v, nxt_v, t_ssem.at[0], t_rsem.at[0], prior_dev)
 
-    @pl.when(has_up)
-    def _():
-        h_up.start()
-
-    @pl.when(has_down)
-    def _():
-        h_down.start()
+    for i in range(half):
+        @pl.when(has_up)
+        def _():
+            h_up[i].start()
+
+        @pl.when(has_down)
+        def _():
+            h_down[i].start()
 
     @pl.when(has_prior)
     def _():
@@ -201,20 +186,18 @@
     local = lax.broadcasted_iota(jnp.int32, (half * crow, flat), 0) + e * (half * crow)
     reads = (jnp.abs(rows - local.astype(jnp.float32)) < 0.5).astype(jnp.float32)
 
-    @pl.when(has_down)
-    def _():
-        h_up.wait_recv()
-
-    @pl.when(has_up)
-    def _():
-        h_down.wait_recv()
-
-    for at in range(3):
-        for pair in range(pairs):
-            slot_at = at * pairs + pair
-            unpack(wide, (at,), pair, h_after[slot_at], h_before[slot_at])
-
-    for i in range(half):
+    for i in range(half):
+        @pl.when(has_down)
+        def _():
+            h_up[i].wait_recv()
+
+        @pl.when(has_up)
+        def _():
+            h_down[i].wait_recv()
+
+        for at in range(3):
+            wide[at, i, crow : crow + 4] = h_after[i, at]
+            wide[at, i, crow + 4 : crow + 8] = h_before[i, at]
         wl, wt = wide[1, i], wide[2, i]
         wl2, wt2 = wl * wl, wt * wt
         coef[i, 0] = 1.0 - wl2 - wt2
@@ -233,18 +216,19 @@
             )
         end_v[i] = wide[0, i, 0:crow]
 
-    e_copy = remote(end_v, prior_v, t_ssem.at[1], t_rsem.at[1], later_dev)
-
-    @pl.when(has_later)
-    def _():
-        e_copy.start()
+        @pl.when(has_later & (i < half // 2))
+        def _():
+            e_copy[i].start()
 
     fhi, flo = split(jnp.concatenate([end_v[i] for i in range(half)], axis=0))
     jh, jl = jhi[...], jlo[...]
-    seen = mm(fhi, jh, NT) + mm(flo, jh, NT) + mm(fhi, jl, NT)
+    rows_own = half * crow
+    both = mm(jnp.concatenate([fhi, flo], axis=0), jh, NT)
+    seen = both[:rows_own] + both[rows_own:] + mm(fhi, jl, NT)
     evolved = jnp.sum(seen * reads, axis=0, keepdims=True)
     whi, wlo = split(reads * (precisions * (evolved - values)))
-    placed = mm(whi, jh, NN) + mm(wlo, jh, NN) + mm(whi, jl, NN)
+    both = mm(jnp.concatenate([whi, wlo], axis=0), jh, NN)
+    placed = both[:rows_own] + both[rows_own:] + mm(whi, jl, NN)
 
     @pl.when(has_later)
     def _():
@@ -331,25 +315,18 @@
     def _():
         a_down.start()
 
-    @pl.when(has_prior)
-    def _():
-        e_copy.wait_recv()
-
-    @pl.when(has_down)
-    def _():
-        a_up.wait_recv()
-
-    @pl.when(has_up)
-    def _():
-        a_down.wait_recv()
-
-    for i in range(half):
-        prec = mp_ref[e * half + i]
-        gap = jnp.zeros((crow - 8, lon), jnp.float32)
-        rims = jnp.concatenate([a_before[i][:, 0:lon], gap, a_after[i][:, 0:lon]], axis=0)
-        grad_v[e * half + i] = adj[i, 0:crow, 0:lon] + rims + prec * (inc_v[i] - prior_v[i, :, 0:lon])
-    g_copy = remote(grad_v.at[own], grad_v.at[own], g_ssem, g_rsem, partner)
-    g_copy.start()
+    for i in range(half):
+        for h in range(E):
+            here = (k == e * half + i) & (e == h)
+
+            @pl.when(jnp.logical_not(here))
+            def _():
+                owner_copy(i, h).wait_send()
+
+    @pl.when(has_later)
+    def _():
+        for i in range(half // 2, half):
+            e_copy[i].start()
 
     p_copy.wait_recv()
     for at in range(T):
@@ -385,6 +362,27 @@
         copy = remote(ca_send, ca_v.at[me], ca_ssem.at[dt * E + de], ca_rsem.at[me], mate(dt, de))
         copy.start()
         ca_copies.append(copy)
+    @pl.when(has_prior)
+    def _():
+        for i in range(half):
+            e_copy[i].wait_recv()
+
+    @pl.when(has_down)
+    def _():
+        a_up.wait_recv()
+
+    @pl.when(has_up)
+    def _():
+        a_down.wait_recv()
+
+    for i in range(half):
+        prec = mp_ref[e * half + i]
+        gap = jnp.zeros((crow - 8, lon), jnp.float32)
+        rims = jnp.concatenate([a_before[i][:, 0:lon], gap, a_after[i][:, 0:lon]], axis=0)
+        grad_v[e * half + i] = adj[i, 0:crow, 0:lon] + rims + prec * (inc_v[i] - prior_v[i, :, 0:lon])
+    g_copy = remote(grad_v.at[own], grad_v.at[own], g_ssem, g_rsem, partner)
+    g_copy.start()
+
     for dt, de in group:
         it = lax.rem(k + dt, T) * E + lax.rem(e + de, E)
         remote(ca_send, ca_v.at[it], ca_ssem.at[0], ca_rsem.at[it], partner).wait_recv()
@@ -405,12 +403,14 @@
         remote(cb_send, cb_v.at[it], cb_ssem.at[0], cb_rsem.at[it], partner).wait_recv()
     @pl.when(has_up)
     def _():
-        h_up.wait_send()
+        for i in range(half):
+            h_up[i].wait_send()
         a_up.wait_send()
 
     @pl.when(has_down)
     def _():
-        h_down.wait_send()
+        for i in range(half):
+            h_down[i].wait_send()
         a_down.wait_send()
 
     @pl.when(has_prior)
@@ -419,18 +419,11 @@
 
     @pl.when(has_later)
     def _():
-        e_copy.wait_send()
+        for i in range(half):
+            e_copy[i].wait_send()
 
     p_copy.wait_send()
     g_copy.wait_send()
-    for i in range(half):
-        for h in range(E):
-            here = (k == e * half + i) & (e == h)
-
-            @pl.when(jnp.logical_not(here))
-            def _():
-                owner_copy(i, h).wait_send()
-
     for i in range(half):
         @pl.when(has_up)
         def _():
@@ -470,7 +463,7 @@
     members = perturbations.shape[0]
     blocks, slots = obs_jacobian.shape[1:3]
     half, width = levels // E, -(-lon // 128) * 128
-    pairs, flat = half // 2, blocks * slots
+    flat = blocks * slots
     f32, dma = jnp.float32, pltpu.SemaphoreType.DMA
     vmem, anyw = pl.BlockSpec(memory_space=pltpu.VMEM), pl.BlockSpec(memory_space=pl.ANY)
 
@@ -493,12 +486,13 @@
             buf(flat, lon),
             buf(flat, width, kind=jnp.bfloat16), buf(flat, width, kind=jnp.bfloat16),
             buf(3, half, 24, width), buf(half, 5, 24, width), buf(half, 24, width),
-            buf(3 * pairs, 8, width), buf(3 * pairs, 8, width), buf(3 * pairs, 8, width), buf(3 * pairs, 8, width),
+            buf(half, 3, 4, width), buf(half, 3, 4, width), buf(half, 3, 4, width), buf(half, 3, 4, width),
             buf(half, 4, width), buf(half, 4, width), buf(half, 4, width), buf(half, 4, width),
             buf(half, crow, width), buf(half, crow, lon), buf(half, crow, width),
             buf(half, E, 8, width), buf(half, 2, 4, width), buf(T, 8, width), buf(T, 4, width),
             buf(8, 128), buf(T * E, 8, 128), buf(8, 128),
-            dma((10,)), dma((2,)), dma((2,)), dma((2,)), dma((2,)), dma((2,)), dma((2,)), dma, dma,
+            dma((10,)), dma((2, half)), dma((2, half)), dma((2,)), dma((2,)), dma((1,)), dma((1,)),
+            dma((half,)), dma((half,)), dma, dma,
             dma((half, E)), dma((T,)), dma((half, 2)), dma((T,)),
             dma((T * E,)), dma((T * E,)), dma((L,)), dma((L,)), dma, dma,
         ],

time: 28.3 us -> 27 us (0.954)
  Pallas kernels: 27.5 us -> 26.2 us
    pallas_call x1, Pallas kernels: 26.6 us -> 25.2 us  [on_device(): pl.pallas_call(functools.partial(kernel, T, L, E), out_shape=(buf(levels,...]
where the time goes in v3:
time: 27 us; the launch traced here: 26.8 us
  Pallas kernels  26.2 us (97%)
  between operations  0.64 us (2%)
    pallas_call x1, Pallas kernels, on_device(): pl.pallas_call(functools.partial(kernel, T, L, E), out_shape=(buf(levels,...  25.2 us
    pallas_call x1, Pallas kernels, on_device(): pl.pallas_call(functools.partial(finish, L), out_shape=(jax.ShapeDtypeStr...  0.94 us

profile of v3, /device:TPU:0, one launch (start us, length us, event | category | flops | bytes accessed | tf_op | source)
XLA Modules:
  0.0 26.8 jit_solution(10946669984124415786)
XLA Ops:
  0.6 25.2 %shard_map.113 = (f32[4,16,1440]{2,1,0:T(8,128)S(1)}, f32[2,16,2,8,1440]{4,3,2,1,0:T(8,128)S(1)}, f32[4,8,128]{2,1,0:T(8,128)S(1)}) custom-call(s32[1,32]{1,0:T(1,128)} %rows_hbm.1, s32[1,32]{1,0:T(1,128)} %cnt_hbm.1, f32[16,32]{1,0:T(8,128)} %bitcast.18, f32[16,32]{1,0:T(8,128)} %bitcast.19, f32[4]{0:T(128)} %mp_hbm.1, f32[4,16,1440]{2,1,0:T(8,128)} %bitcast.15, ...), custom_call_target="tpu_custom_call" | custom-call | tf_op jit(solution)/shard_map/pallas_call | solution.py:473
  25.9 0.9 %shard_map.114 = (f32[4,16,1440]{2,1,0:T(8,128)}, f32[16,1440]{1,0:T(8,128)}) custom-call(f32[4,16,1440]{2,1,0:T(8,128)S(1)} %get-tuple-element.7.grad_v, f32[2,16,2,8,1440]{4,3,2,1,0:T(8,128)S(1)} %get-tuple-element.8.pert_v, f32[4,8,128]{2,1,0:T(8,128)S(1)} %get-tuple-element.9.cb_v), custom_call_target="tpu_custom_call" | custom-call | tf_op jit(solution)/shard_map/pallas_call | solution.py:508

commit v4 on v3

--- a/solution.py
+++ b/solution.py
@@ -48,7 +48,7 @@
     h_first, h_last, h_after, h_before, a_up_v, a_down_v, a_after, a_before,
     end_v, nxt_v, prior_v, forc, edge, rs_v, edge_v, ca_send, ca_v, cb_send,
     load_sem, h_ssem, h_rsem, a_ssem, a_rsem, t_ssem, t_rsem, e_ssem, e_rsem, p_ssem, p_rsem,
-    rs_ssem, rs_rsem, ed_ssem, ed_rsem, ca_ssem, ca_rsem, cb_ssem, cb_rsem, g_ssem, g_rsem,
+    rs_ssem, rs_rsem, ed_ssem, ed_rsem, ca_ssem, ca_rsem, cb_ssem, cb_rsem, g_ssem, g_rsem, all_sem,
 ):
     k, b, e = lax.axis_index("tm"), lax.axis_index("lat"), lax.axis_index("ens")
     half, crow, lon = inc_v.shape
@@ -71,10 +71,11 @@
         pltpu.make_async_copy(prc_hbm, prc_ref, load_sem.at[8]),
         pltpu.make_async_copy(mp_hbm, mp_ref, load_sem.at[9]),
     ]
-    for item in loads:
+    for item in loads[:3]:
         item.start()
 
     barrier = pltpu.get_barrier_semaphore()
+    direct = T * L * E <= 64
     group = [(dt, de) for dt in range(T) for de in range(E) if dt or de]
 
     def mate(dt, de):
@@ -100,6 +101,8 @@
 
     for item in loads[:3]:
         item.wait()
+    for item in loads[4:5] + loads[3:4] + loads[5:]:
+        item.start()
     for at, ref in enumerate((inc_v, wlon_v, wlat_v)):
         for i in range(half):
             wide[at, i, 0:16, 0:lon] = ref[i]
@@ -108,6 +111,9 @@
             h_last[i, at] = wide[at, i, crow - 4 : crow]
 
     pl.semaphore_wait(barrier, len(group) + L - 1)
+    if direct:
+        for db in range(1, L):
+            pl.semaphore_signal(all_sem, inc=1, device_id={"lat": lax.rem(b + db, L)}, device_id_type=MESH)
 
     h_up = [remote(h_last.at[i], h_before.at[i], h_ssem.at[0, i], h_rsem.at[0, i], up) for i in range(half)]
     h_down = [remote(h_first.at[i], h_after.at[i], h_ssem.at[1, i], h_rsem.at[1, i], down) for i in range(half)]
@@ -354,14 +360,28 @@
     for m in range(E * members):
         dots = jnp.sum(pert_v[m // members, m % members, e] * total, axis=1, keepdims=True)
         part = jnp.where(lane == m, dots, part)
+    part = jnp.sum(part, axis=0, keepdims=True)
     ca_send[...] = part
-    me = k * E + e
-    ca_v[me] = part
-    ca_copies = []
-    for dt, de in group:
-        copy = remote(ca_send, ca_v.at[me], ca_ssem.at[dt * E + de], ca_rsem.at[me], mate(dt, de))
+    if direct:
+        crowd = [(dt, db, de) for dt in range(T) for db in range(L) for de in range(E) if dt or db or de]
+        pl.semaphore_wait(all_sem, L - 1)
+    else:
+        crowd = [(dt, 0, de) for dt, de in group]
+
+    def seat(dt, db, de):
+        at, lat, ens = lax.rem(k + dt, T), lax.rem(b + db, L), lax.rem(e + de, E)
+        index = (at * L + lat) * E + ens if direct else at * E + ens
+        return index, {"tm": at, "lat": lat, "ens": ens}
+
+    sums = cb_v if direct else ca_v
+    me, _ = seat(0, 0, 0)
+    sums[me] = part
+    coef_copies = []
+    for at, (dt, db, de) in enumerate(crowd):
+        copy = remote(ca_send, sums.at[me], ca_ssem.at[at], ca_rsem.at[me], seat(dt, db, de)[1])
         copy.start()
-        ca_copies.append(copy)
+        coef_copies.append(copy)
+
     @pl.when(has_prior)
     def _():
         for i in range(half):
@@ -382,25 +402,24 @@
         grad_v[e * half + i] = adj[i, 0:crow, 0:lon] + rims + prec * (inc_v[i] - prior_v[i, :, 0:lon])
     g_copy = remote(grad_v.at[own], grad_v.at[own], g_ssem, g_rsem, partner)
     g_copy.start()
-
-    for dt, de in group:
-        it = lax.rem(k + dt, T) * E + lax.rem(e + de, E)
-        remote(ca_send, ca_v.at[it], ca_ssem.at[0], ca_rsem.at[it], partner).wait_recv()
-    part = ca_v[0]
-    for at in range(1, T * E):
-        part = part + ca_v[at]
-    cb_send[...] = part
-    cb_v[b] = part
-    cb_copies = []
-    for db in range(1, L):
-        copy = remote(cb_send, cb_v.at[b], cb_ssem.at[db], cb_rsem.at[b], {"lat": lax.rem(b + db, L)})
-        copy.start()
-        cb_copies.append(copy)
-
+    for dt, db, de in crowd:
+        it, _ = seat(dt, db, de)
+        remote(ca_send, sums.at[it], ca_ssem.at[0], ca_rsem.at[it], partner).wait_recv()
+    if not direct:
+        part = ca_v[0]
+        for at in range(1, T * E):
+            part = part + ca_v[at]
+        cb_send[...] = part
+        cb_v[b] = part
+        for db in range(1, L):
+            copy = remote(cb_send, cb_v.at[b], cb_ssem.at[db], cb_rsem.at[b], {"lat": lax.rem(b + db, L)})
+            copy.start()
+            coef_copies.append(copy)
+        for db in range(1, L):
+            it = lax.rem(b + db, L)
+            remote(cb_send, cb_v.at[it], cb_ssem.at[0], cb_rsem.at[it], partner).wait_recv()
     g_copy.wait_recv()
-    for db in range(1, L):
-        it = lax.rem(b + db, L)
-        remote(cb_send, cb_v.at[it], cb_ssem.at[0], cb_rsem.at[it], partner).wait_recv()
+
     @pl.when(has_up)
     def _():
         for i in range(half):
@@ -433,19 +452,19 @@
         def _():
             edge_down[i].wait_send()
 
-    for copy in ca_copies + cb_copies:
+    for copy in coef_copies:
         copy.wait_send()
 
 
-def finish(L, grad_v, pert_v, cb_v, grad_hbm, step_hbm, step_v, out_sem):
+def finish(grad_v, pert_v, cb_v, grad_hbm, step_hbm, step_v, out_sem):
     g_out = pltpu.make_async_copy(grad_v, grad_hbm, out_sem.at[0])
     g_out.start()
     ens, members, rows, _, lon = pert_v.shape
     count = ens * members
     part = cb_v[0]
-    for at in range(1, L):
+    for at in range(1, cb_v.shape[0]):
         part = part + cb_v[at]
-    factor = jnp.broadcast_to(jnp.sum(part, axis=0, keepdims=True), (8, 128)) * (-1.0 / (count - 1.0))
+    factor = jnp.broadcast_to(part, (8, 128)) * (-1.0 / (count - 1.0))
     for h in range(rows):
         mixed = jnp.zeros((8, lon), jnp.float32)
         for m in range(count):
@@ -464,6 +483,7 @@
     blocks, slots = obs_jacobian.shape[1:3]
     half, width = levels // E, -(-lon // 128) * 128
     flat = blocks * slots
+    heard, spoken = (T * L * E, T * L * E) if T * L * E <= 64 else (L, T * E)
     f32, dma = jnp.float32, pltpu.SemaphoreType.DMA
     vmem, anyw = pl.BlockSpec(memory_space=pltpu.VMEM), pl.BlockSpec(memory_space=pl.ANY)
 
@@ -475,7 +495,7 @@
         out_shape=(
             buf(levels, crow, lon),
             buf(E, members, crow // 8, 8, lon),
-            buf(L, 8, 128),
+            buf(heard, 1, 128),
         ),
         in_specs=[pl.BlockSpec(memory_space=pltpu.HBM)] * 10,
         out_specs=(vmem, vmem, vmem),
@@ -490,11 +510,11 @@
             buf(half, 4, width), buf(half, 4, width), buf(half, 4, width), buf(half, 4, width),
             buf(half, crow, width), buf(half, crow, lon), buf(half, crow, width),
             buf(half, E, 8, width), buf(half, 2, 4, width), buf(T, 8, width), buf(T, 4, width),
-            buf(8, 128), buf(T * E, 8, 128), buf(8, 128),
+            buf(1, 128), buf(T * E, 1, 128), buf(1, 128),
             dma((10,)), dma((2, half)), dma((2, half)), dma((2,)), dma((2,)), dma((1,)), dma((1,)),
             dma((half,)), dma((half,)), dma, dma,
             dma((half, E)), dma((T,)), dma((half, 2)), dma((T,)),
-            dma((T * E,)), dma((T * E,)), dma((L,)), dma((L,)), dma, dma,
+            dma((spoken,)), dma((spoken,)), dma((L,)), dma((L,)), dma, dma, pltpu.SemaphoreType.REGULAR,
         ],
         compiler_params=pltpu.CompilerParams(
             collective_id=0, has_side_effects=True, vmem_limit_bytes=56 * 1024 * 1024
@@ -506,7 +526,7 @@
         perturbations.reshape(members, crow // 8, 8, lon),
     )
     grad, step = pl.pallas_call(
-        functools.partial(finish, L),
+        finish,
         out_shape=(
             jax.ShapeDtypeStruct((levels, crow, lon), f32),
             jax.ShapeDtypeStruct((crow, lon), f32),

time: 27 us -> 25.2 us (0.933)
  Pallas kernels: 26.2 us -> 24.4 us
    pallas_call x1, Pallas kernels: 25.2 us -> 23.4 us  [on_device(): pl.pallas_call(functools.partial(kernel, T, L, E), out_shape=(buf(levels,...]
where the time goes in v4:
time: 25.2 us; the launch traced here: 25 us
  Pallas kernels  24.4 us (97%)
  between operations  0.64 us (3%)
    pallas_call x1, Pallas kernels, on_device(): pl.pallas_call(functools.partial(kernel, T, L, E), out_shape=(buf(levels,...  23.4 us
    pallas_call x1, Pallas kernels, on_device(): pl.pallas_call(finish, out_shape=(jax.ShapeDtypeStruct((levels, crow, lon...  0.97 us

profile of v4, /device:TPU:0, one launch (start us, length us, event | category | flops | bytes accessed | tf_op | source)
XLA Modules:
  0.0 25.0 jit_solution(12748324928047681941)
XLA Ops:
  0.6 23.4 %shard_map.113 = (f32[4,16,1440]{2,1,0:T(8,128)S(1)}, f32[2,16,2,8,1440]{4,3,2,1,0:T(8,128)S(1)}, f32[32,1,128]{2,1,0:T(1,128)S(1)}) custom-call(s32[1,32]{1,0:T(1,128)} %rows_hbm.1, s32[1,32]{1,0:T(1,128)} %cnt_hbm.1, f32[16,32]{1,0:T(8,128)} %bitcast.18, f32[16,32]{1,0:T(8,128)} %bitcast.19, f32[4]{0:T(128)} %mp_hbm.1, f32[4,16,1440]{2,1,0:T(8,128)} %bitcast.15, ...), custom_call_target="tpu_custom_call" | custom-call | tf_op jit(solution)/shard_map/pallas_call | solution.py:493
  24.1 1.0 %shard_map.114 = (f32[4,16,1440]{2,1,0:T(8,128)}, f32[16,1440]{1,0:T(8,128)}) custom-call(f32[4,16,1440]{2,1,0:T(8,128)S(1)} %get-tuple-element.7.grad_v, f32[2,16,2,8,1440]{4,3,2,1,0:T(8,128)S(1)} %get-tuple-element.8.pert_v, f32[32,1,128]{2,1,0:T(1,128)S(1)} %get-tuple-element.9.cb_v), custom_call_target="tpu_custom_call" | custom-call | tf_op jit(solution)/shard_map/pallas_call | solution.py:528
